TPU v7x, 32 devices: a whole 2x2x4 slice. The times are simulated.
32 devices in a mesh: rep: 4 (over x, core), shard: 8 (over z, y).
Axes of the slice: x: 2, y: 2, z: 4, core: 2. Of those that a mesh axis runs over, the one named last changes fastest.
Arguments:
- outer_delta: float32 [4, 2097152], P('rep', 'shard'), may hold values from -40 to 40
- offsets: int32 [65], replicated, may hold values from 0 to 2097152, as said below
- parameters: float32 [2097152], P('shard'), may hold values from -6 to 6
- momentum: float32 [2097152], P(('shard', 'rep')), may hold values from -1.2 to 1.2
Outputs:
- new_parameters: float32 [2097152], P('shard')
- new_momentum: float32 [2097152], P(('shard', 'rep'))
Inputs may be any that keep to these rules, and one draw needn't show every extreme that they name: `offsets`: strictly increasing multiples of 128, the first 0 and the last 2097152.
All inputs are finite; a program needn't handle non-finite values.
Results may differ from a plain program's by a relative error of at most 0.0003.
Values sent between devices are 32-bit elements; how exact they have to be, the bound alone decides.
A program may use at most 64 MiB of HBM per device.

v0:
```python
import math
import jax
import jax.numpy as jnp
from jax import lax
from jax.sharding import PartitionSpec as P

LR_OUTER = 0.7
MU_OUTER = 0.9
CLIP_RMS = 0.1
EPSILON = 1e-06


def one_hot_rows(first_pos, block_len, offsets):
    tensors = offsets.shape[0] - 1
    positions = first_pos + jnp.arange(block_len, dtype=jnp.int32)
    segment = jnp.sum((positions[:, None] >= offsets[None, 1:tensors]).astype(jnp.int32), axis=1)
    return (segment[:, None] == jnp.arange(tensors, dtype=jnp.int32)[None, :]).astype(jnp.float32)


def tensor_squares(values, first_pos, offsets):
    total_len = values.shape[0]
    block_len = math.gcd(total_len, 8192)
    value_rows = values.reshape(total_len // block_len, block_len)
    block_starts = first_pos + jnp.arange(total_len // block_len, dtype=jnp.int32) * block_len

    def partial_squares(items):
        row_values, row_start = items
        selector = one_hot_rows(row_start, block_len, offsets)
        return jnp.dot(
            row_values * row_values,
            selector,
            precision=lax.Precision.HIGHEST,
            preferred_element_type=jnp.float32,
        )

    return jnp.sum(lax.map(partial_squares, (value_rows, block_starts)), axis=0)


def element_factor(factor, total_len, first_pos, offsets):
    block_len = math.gcd(total_len, 8192)
    block_starts = first_pos + jnp.arange(total_len // block_len, dtype=jnp.int32) * block_len

    def spread_factor(row_start):
        selector = one_hot_rows(row_start, block_len, offsets)
        return jnp.dot(
            selector, factor, precision=lax.Precision.HIGHEST, preferred_element_type=jnp.float32
        )

    return lax.map(spread_factor, block_starts).reshape(total_len)


def clip_factor(squares_sum, offsets):
    lengths = (offsets[1:] - offsets[:-1]).astype(jnp.float32)
    return jnp.minimum(1.0, CLIP_RMS * jnp.sqrt(lengths) * lax.rsqrt(squares_sum + EPSILON))


def on_device(outer_delta, offsets, parameters, momentum):
    replicas = lax.axis_size("rep")
    shard_len = parameters.shape[0]
    own_len = shard_len // replicas
    rep_index = lax.axis_index("rep")
    shard_start = lax.axis_index("shard") * shard_len
    local_delta = outer_delta.reshape(shard_len)
    avg_delta = lax.psum_scatter(local_delta, "rep", scatter_dimension=0, tiled=True) / jnp.float32(
        replicas
    )
    first_pos = shard_start + rep_index * own_len
    squares_sum = lax.psum(tensor_squares(avg_delta, first_pos, offsets), ("shard", "rep"))
    factor = clip_factor(squares_sum, offsets)
    scaled = avg_delta * element_factor(factor, own_len, first_pos, offsets)
    owned_params = lax.dynamic_slice_in_dim(parameters, rep_index * own_len, own_len)
    new_momentum = MU_OUTER * momentum + scaled
    new_owned = owned_params - LR_OUTER * (scaled + MU_OUTER * new_momentum)
    new_parameters = lax.all_gather(new_owned, "rep", axis=0, tiled=True)
    return (new_parameters, new_momentum)


def solution(mesh):
    return jax.shard_map(
        on_device,
        mesh=mesh,
        in_specs=(P("rep", "shard"), P(), P("shard"), P(("shard", "rep"))),
        out_specs=(P("shard"), P(("shard", "rep"))),
        check_vma=False,
    )
```

profile of v0, /device:TPU:0, one launch (start us, length us, event | category | flops | bytes accessed | tf_op | source)
XLA Modules:
  0.0 162.3 jit_solution(8617485549905927681)
XLA Ops:
  7.2 0.7 all-reduce.3.cloned.1.call-update
  8.0 0.7 dynamic-slice
  9.4 40.0 %all-reduce.3.cloned.1.call-done = f32[262144]{0:T(1024)} async-done(((f32[262144]{0:T(1024)}), f32[262144]{0:T(1024)}) %all-reduce.3.cloned.1.call-update) | async-done | bytes 1048592
  49.4 1.0 dynamic-slice_multiply_fusion
  50.4 23.2 %while.20 = (s32[]{:T(128)}, f32[8,64]{1,0:T(8,128)S(1)}, f32[8,8192]{1,0:T(8,128)S(1)}, s32[8]{0:T(128)S(1)}, s32[65]{0:T(128)S(1)}, /*index=5*/s32[]{:T(128)}, s32[]{:T(128)}) while((s32[]{:T(128)}, f32[8,64]{1,0:T(8,128)S(1)}, f32[8,8192]{1,0:T(8,128)S(1)}, s32[8]{0:T(128)S(1)}, s32[65]{0:T(128)S(1)}, /*index=5*/s32[]{:T(128)}, ...), condition=%wide.region_3.4_spmd, body=%wide.region_1.3_spmd.sunk | while | flops 8372226 | bytes 165465 | solution.py:36
  50.5 0.7 dynamic_slice.24
  51.1 0.7 iota_add_fusion.4
  52.2 1.1 fusion.10
  53.4 0.7 dynamic_slice.24
  54.0 0.7 iota_add_fusion.4
  55.1 1.1 fusion.10
  56.3 0.7 dynamic_slice.24
  56.9 0.7 iota_add_fusion.4
  58.0 1.1 fusion.10
  59.2 0.7 dynamic_slice.24
  59.8 0.7 iota_add_fusion.4
  60.9 1.1 fusion.10
  62.1 0.7 dynamic_slice.24
  62.7 0.7 iota_add_fusion.4
  63.8 1.1 fusion.10
  65.0 0.7 dynamic_slice.24
  65.6 0.7 iota_add_fusion.4
  66.8 1.1 fusion.10
  67.9 0.7 dynamic_slice.24
  68.5 0.7 iota_add_fusion.4
  69.7 1.1 fusion.10
  70.8 0.7 dynamic_slice.24
  71.4 0.7 iota_add_fusion.4
  72.6 1.1 fusion.10
  73.7 39.8 %psum.7 = f32[64]{0:T(128)S(1)} all-reduce(f32[64]{0:T(128)S(1)} %reduce_sum.27), channel_id=1, replica_groups=mesh['rep'=4,'shard'=8] {'shard','rep'}, use_global_device_ids=true, to_apply=%region_5.6 | all-reduce | flops 64 | bytes 512 | tf_op jit(solution)/shard_map/psum | solution.py:68
  113.6 20.5 %while.21 = (s32[]{:T(128)}, f32[8,8192]{1,0:T(8,128)S(1)}, s32[8]{0:T(128)S(1)}, s32[65]{0:T(128)S(1)}, f32[64]{0:T(128)S(1)}, /*index=5*/s32[]{:T(128)}, s32[]{:T(128)}) while((s32[]{:T(128)}, f32[8,8192]{1,0:T(8,128)S(1)}, s32[8]{0:T(128)S(1)}, s32[65]{0:T(128)S(1)}, f32[64]{0:T(128)S(1)}, /*index=5*/s32[]{:T(128)}, s32[]{:T(128)}) %tuple.50), condition=%wide.region_8.9_spmd, body=%wide.region_6.8_spmd.sunk | while | flops 8364034 | bytes 230485 | solution.py:49
  114.2 0.6 iota_add_fusion.5
  115.2 0.7 fusion.12
  116.7 0.6 iota_add_fusion.5
  117.8 0.7 fusion.12
  119.3 0.6 iota_add_fusion.5
  120.4 0.7 fusion.12
  122.9 0.7 fusion.12
  124.4 0.6 iota_add_fusion.5
  125.5 0.7 fusion.12
  128.1 0.7 fusion.12
  129.6 0.6 iota_add_fusion.5
  130.6 0.7 fusion.12
  132.1 0.6 iota_add_fusion.5
  133.2 0.7 fusion.12
  134.2 1.9 %multiply_subtract_fusion = (f32[65536]{0:T(1024)}, f32[65536]{0:T(1024)}) fusion(f32[262144]{0:T(1024)} %param.10, s32[]{:T(128)S(6)} %select_n.3, f32[65536]{0:T(1024)S(1)} %copy-done, f32[65536]{0:T(1024)S(1)} %bitcast.24, f32[262144]{0:T(1024)} %all-reduce.3.cloned.1.call-done, u32[]{:T(128)S(6)} %multiply.2), kind=kLoop, calls=%fused_computation.15 | loop fusion | flops 524288 | bytes 1572872 | tf_op jit(solution)/shard_map/sub | solution.py:73
  136.1 17.0 %all-gather.2.cloned.1.call-done = f32[262144]{0:T(1024)} async-done(((f32[65536]{0:T(1024)}), f32[262144]{0:T(1024)}) %all-gather.2.cloned.1.call-update) | async-done | bytes 1048592 | tf_op jit(solution)/shard_map/all_gather | solution.py:74
  153.2 2.3 %copy.24 = f32[262144]{0:T(1024)} copy(f32[262144]{0:T(1024)} %all-gather.2.cloned.1.call-done) | data formatting | bytes 2097152
  (74 shorter events, 14.2 us)
Async XLA Ops:
  7.2 0.8 copy-start.2
  7.2 42.2 %all-reduce.3.cloned.1.call-start = ((), (), s32[]{:S(2)}) async-start(), calls=%async_computation.1 | async-start | bytes 2097152
  7.2 43.2 %copy-start.1 = (s32[65]{0:T(128)S(1)}, s32[65]{0:T(128)}, u32[]{:S(2)}) copy-start(s32[65]{0:T(128)} %param.9) | copy-start | bytes 784
  7.9 145.3 %all-gather.2.cloned.1.call-start = ((), (), s32[]{:S(2)}) async-start(), calls=%async_computation | async-start | bytes 1310720 | tf_op jit(solution)/shard_map/all_gather | solution.py:74
  113.6 20.6 %copy-start = (f32[65536]{0:T(1024)S(1)}, f32[65536]{0:T(1024)}, u32[]{:S(2)}) copy-start(f32[65536]{0:T(1024)} %param.11) | copy-start | bytes 786436
Sparse Core Ops, SparseCore 0:
  10.3 39.0 all-reduce.2
  136.3 16.8 all-gather.1
where the time goes:
time: 163 us; the launch traced here: 162 us
  waiting for transfers between devices  57.7 us (35%)
  blocking collectives  39.8 us (24%)
  other arithmetic  19.1 us (12%)
  local copies, waits for them, and re-layouts  15.6 us (10%)
  between operations  14.9 us (9%)
  matrix products  14.5 us (9%)
    unnamed x3, waiting for transfers between devices  40.7 us
    psum x1, blocking collectives, on_device(): lax.psum(tensor_squares(avg_delta, first_pos, offsets), ('shard', 'rep'))  39.8 us
    all_gather x1, waiting for transfers between devices, on_device(): new_parameters = lax.all_gather(new_owned, 'rep', axis=0, tiled=True)  17 us
    add x16, other arithmetic, one_hot_rows(): positions = first_pos + jnp.arange(block_len, dtype=jnp.int32)  10.7 us
    dynamic_slice x16, local copies, waits for them, and re-layouts, tensor_squares(): return jnp.sum(lax.map(partial_squares, (value_rows, block_starts)), axis=0)  10 us
    dot_general x8, matrix products, partial_squares(): jnp.dot(row_values * row_values, selector, precision=lax.Precision.HIGHES...  8.58 us
    dot_general x8, matrix products, spread_factor(): jnp.dot(selector, factor, precision=lax.Precision.HIGHEST, preferred_elem...  5.97 us
    reduce_sum x16, other arithmetic, one_hot_rows(): jnp.sum((positions[:, None] >= offsets[None, 1:tensors]).astype(jnp.int32...  5.37 us
  transfers between devices with their start and end apart: 2, of which 2 were waited for; matrix products, arithmetic and copies ran while one was open for 0% of the time, Pallas kernels for 0%

commit v1 on v0

--- a/solution.py
+++ b/solution.py
@@ -71,7 +71,12 @@
     owned_params = lax.dynamic_slice_in_dim(parameters, rep_index * own_len, own_len)
     new_momentum = MU_OUTER * momentum + scaled
     new_owned = owned_params - LR_OUTER * (scaled + MU_OUTER * new_momentum)
-    new_parameters = lax.all_gather(new_owned, "rep", axis=0, tiled=True)
+    ring = [new_owned]
+    for hop in range(3):
+        ring.append(lax.ppermute(ring[-1], "rep", [(dev, (dev + 1) % 4) for dev in range(4)]))
+    new_parameters = jnp.roll(
+        jnp.concatenate(ring[::-1], axis=0), (lax.axis_index("rep") + 1) * ring[0].shape[0], axis=0
+    )
     return (new_parameters, new_momentum)
 
 

time: 163 us -> 162 us (level)
    ppermute x0 -> x3, waiting for transfers between devices: none -> 17.4 us  [on_device(): lax.ppermute(ring[-1], 'rep', [(dev, (dev + 1) % 4) for dev in range(4)])]
    all_gather x1 -> x0, waiting for transfers between devices: 17 us -> none  [on_device(): new_parameters = lax.all_gather(new_owned, 'rep', axis=0, tiled=True)]
    unnamed x3 -> x2, waiting for transfers between devices: 40.7 us -> 40.1 us
  transfers between devices with their start and end apart: 2 -> 4, of which waited for: 2 -> 4; matrix products, arithmetic and copies ran while one was open for 0% -> 1% of each run, Pallas kernels for 0% -> 0%
where the time goes in v1:
time: 162 us; the launch traced here: 161 us
  waiting for transfers between devices  57.5 us (35%)
  blocking collectives  39.8 us (25%)
  other arithmetic  19 us (12%)
  local copies, waits for them, and re-layouts  15.2 us (9%)
  between operations  14.9 us (9%)
  matrix products  14.5 us (9%)
    unnamed x2, waiting for transfers between devices  40.1 us
    psum x1, blocking collectives, on_device(): lax.psum(tensor_squares(avg_delta, first_pos, offsets), ('shard', 'rep'))  39.8 us
    ppermute x3, waiting for transfers between devices, on_device(): lax.ppermute(ring[-1], 'rep', [(dev, (dev + 1) % 4) for dev in range(4)])  17.4 us
    add x16, other arithmetic, one_hot_rows(): positions = first_pos + jnp.arange(block_len, dtype=jnp.int32)  10.7 us
    dynamic_slice x16, local copies, waits for them, and re-layouts, tensor_squares(): return jnp.sum(lax.map(partial_squares, (value_rows, block_starts)), axis=0)  10 us
    dot_general x8, matrix products, partial_squares(): jnp.dot(row_values * row_values, selector, precision=lax.Precision.HIGHES...  8.58 us
    dot_general x8, matrix products, spread_factor(): jnp.dot(selector, factor, precision=lax.Precision.HIGHEST, preferred_elem...  5.97 us
    reduce_sum x16, other arithmetic, one_hot_rows(): jnp.sum((positions[:, None] >= offsets[None, 1:tensors]).astype(jnp.int32...  5.34 us
  transfers between devices with their start and end apart: 4, of which 4 were waited for; matrix products, arithmetic and copies ran while one was open for 1% of the time, Pallas kernels for 0%

profile of v1, /device:TPU:0, one launch (start us, length us, event | category | flops | bytes accessed | tf_op | source)
XLA Modules:
  0.0 161.5 jit_solution(1326695244506626226)
XLA Ops:
  7.2 0.7 all-reduce.3.cloned.1.call-update
  8.0 1.3 dynamic-slice
  10.0 39.4 %all-reduce.3.cloned.1.call-done = f32[262144]{0:T(1024)} async-done(((f32[262144]{0:T(1024)}), f32[262144]{0:T(1024)}) %all-reduce.3.cloned.1.call-update) | async-done | bytes 1048592
  49.4 1.0 dynamic-slice_multiply_fusion
  50.4 23.2 %while.20 = (s32[]{:T(128)}, f32[8,64]{1,0:T(8,128)S(1)}, f32[8,8192]{1,0:T(8,128)S(1)}, s32[8]{0:T(128)S(1)}, s32[65]{0:T(128)S(1)}, /*index=5*/s32[]{:T(128)}, s32[]{:T(128)}) while((s32[]{:T(128)}, f32[8,64]{1,0:T(8,128)S(1)}, f32[8,8192]{1,0:T(8,128)S(1)}, s32[8]{0:T(128)S(1)}, s32[65]{0:T(128)S(1)}, /*index=5*/s32[]{:T(128)}, ...), condition=%wide.region_3.4_spmd, body=%wide.region_1.3_spmd.sunk | while | flops 8372226 | bytes 165473 | solution.py:36
  50.5 0.7 dynamic_slice.29
  51.2 0.7 iota_add_fusion.4
  52.2 1.1 fusion.10
  53.4 0.7 dynamic_slice.29
  54.1 0.7 iota_add_fusion.4
  55.1 1.1 fusion.10
  56.3 0.7 dynamic_slice.29
  57.0 0.7 iota_add_fusion.4
  58.0 1.1 fusion.10
  59.2 0.7 dynamic_slice.29
  59.9 0.7 iota_add_fusion.4
  60.9 1.1 fusion.10
  62.1 0.7 dynamic_slice.29
  62.8 0.7 iota_add_fusion.4
  63.8 1.1 fusion.10
  65.0 0.7 dynamic_slice.29
  65.7 0.7 iota_add_fusion.4
  66.7 1.1 fusion.10
  67.9 0.7 dynamic_slice.29
  68.6 0.7 iota_add_fusion.4
  69.6 1.1 fusion.10
  70.8 0.7 dynamic_slice.29
  71.5 0.7 iota_add_fusion.4
  72.5 1.1 fusion.10
  73.7 39.8 %psum.7 = f32[64]{0:T(128)S(1)} all-reduce(f32[64]{0:T(128)S(1)} %reduce_sum.27), channel_id=1, replica_groups=mesh['rep'=4,'shard'=8] {'shard','rep'}, use_global_device_ids=true, to_apply=%region_5.6 | all-reduce | flops 64 | bytes 512 | tf_op jit(solution)/shard_map/psum | solution.py:68
  113.5 20.5 %while.21 = (s32[]{:T(128)}, f32[8,8192]{1,0:T(8,128)S(1)}, s32[8]{0:T(128)S(1)}, s32[65]{0:T(128)S(1)}, f32[64]{0:T(128)S(1)}, /*index=5*/s32[]{:T(128)}, s32[]{:T(128)}) while((s32[]{:T(128)}, f32[8,8192]{1,0:T(8,128)S(1)}, s32[8]{0:T(128)S(1)}, s32[65]{0:T(128)S(1)}, f32[64]{0:T(128)S(1)}, /*index=5*/s32[]{:T(128)}, s32[]{:T(128)}) %tuple.46), condition=%wide.region_8.9_spmd, body=%wide.region_6.8_spmd.sunk | while | flops 8364034 | bytes 230493 | solution.py:49
  114.2 0.6 iota_add_fusion.5
  115.2 0.7 fusion.12
  117.8 0.7 fusion.12
  119.3 0.6 iota_add_fusion.5
  120.3 0.7 fusion.12
  121.9 0.6 iota_add_fusion.5
  122.9 0.7 fusion.12
  124.5 0.6 iota_add_fusion.5
  125.5 0.7 fusion.12
  128.0 0.7 fusion.12
  130.6 0.7 fusion.12
  133.2 0.7 fusion.12
  134.1 1.8 %multiply_subtract_fusion = (f32[65536]{0:T(1024)S(1)}, f32[65536]{0:T(1024)}) fusion(f32[262144]{0:T(1024)} %param.10, s32[]{:T(128)S(6)} %select_n.16, f32[65536]{0:T(1024)S(1)} %copy-done, f32[65536]{0:T(1024)S(1)} %bitcast.24, f32[262144]{0:T(1024)} %all-reduce.3.cloned.1.call-done, u32[]{:T(128)S(6)} %multiply.2), kind=kLoop, calls=%fused_computation.15 | loop fusion | flops 524288 | bytes 1572872 | tf_op jit(solution)/shard_map/sub | solution.py:73
  136.0 5.8 %collective-permute-done = f32[65536]{0:T(1024)S(1)} collective-permute-done((f32[65536]{0:T(1024)S(1)}, f32[65536]{0:T(1024)S(1)}, u32[]{:S(2)}, u32[]{:S(2)}) %collective-permute-start) | collective-permute-done | bytes 262176 | tf_op jit(solution)/shard_map/ppermute | solution.py:76
  141.8 5.8 %collective-permute-done.1 = f32[65536]{0:T(1024)S(1)} collective-permute-done((f32[65536]{0:T(1024)S(1)}, f32[65536]{0:T(1024)S(1)}, u32[]{:S(2)}, u32[]{:S(2)}) %collective-permute-start.1) | collective-permute-done | bytes 262176 | tf_op jit(solution)/shard_map/ppermute | solution.py:76
  147.6 5.8 %collective-permute-done.2 = f32[65536]{0:T(1024)S(1)} collective-permute-done((f32[65536]{0:T(1024)S(1)}, f32[65536]{0:T(1024)S(1)}, u32[]{:S(2)}, u32[]{:S(2)}) %collective-permute-start.2) | collective-permute-done | bytes 262176 | tf_op jit(solution)/shard_map/ppermute | solution.py:76
  153.6 1.0 dynamic_slice.19
  (83 shorter events, 15.6 us)
Async XLA Ops:
  7.2 43.3 %copy-start.1 = (s32[65]{0:T(128)S(1)}, s32[65]{0:T(128)}, u32[]{:S(2)}) copy-start(s32[65]{0:T(128)} %param.9) | copy-start | bytes 784
  7.2 42.2 %all-reduce.3.cloned.1.call-start = ((), (), s32[]{:S(2)}) async-start(), calls=%async_computation | async-start | bytes 2097152
  73.7 60.5 %copy-start = (f32[65536]{0:T(1024)S(1)}, f32[65536]{0:T(1024)}, u32[]{:S(2)}) copy-start(f32[65536]{0:T(1024)} %param.11) | copy-start | bytes 786436
  136.0 5.8 %collective-permute-start = (f32[65536]{0:T(1024)S(1)}, f32[65536]{0:T(1024)S(1)}, u32[]{:S(2)}, u32[]{:S(2)}) collective-permute-start(f32[65536]{0:T(1024)S(1)} %get-tuple-element.78), channel_id=1, source_target_pairs={{0,8},{8,16},{16,24},{24,0},{1,9},{9,17},{17,25},{25,1},{2,10},{10... | collective-permute-start | bytes 786440 | tf_op jit(solution)/shard_map/ppermute | solution.py:76
  141.8 5.8 %collective-permute-start.1 = (f32[65536]{0:T(1024)S(1)}, f32[65536]{0:T(1024)S(1)}, u32[]{:S(2)}, u32[]{:S(2)}) collective-permute-start(f32[65536]{0:T(1024)S(1)} %collective-permute-done), channel_id=1, source_target_pairs={{0,8},{8,16},{16,24},{24,0},{1,9},{9,17},{17,25},{25,1},{2,10},{10... | collective-permute-start | bytes 786440 | tf_op jit(solution)/shard_map/ppermute | solution.py:76
  147.6 5.8 %collective-permute-start.2 = (f32[65536]{0:T(1024)S(1)}, f32[65536]{0:T(1024)S(1)}, u32[]{:S(2)}, u32[]{:S(2)}) collective-permute-start(f32[65536]{0:T(1024)S(1)} %collective-permute-done.1), channel_id=1, source_target_pairs={{0,8},{8,16},{16,24},{24,0},{1,9},{9,17},{17,25},{25,1},{2,10},{10... | collective-permute-start | bytes 786440 | tf_op jit(solution)/shard_map/ppermute | solution.py:76
Sparse Core Ops, SparseCore 0:
  10.3 39.0 all-reduce.2
